TPU v7x, 32 devices: a whole 2x2x4 slice. The times are simulated.
32 devices in a mesh: groups: 2 (over y), dom: 4 (over z), shot: 4 (over x, core).
Axes of the slice: x: 2, y: 2, z: 4, core: 2. Of those that a mesh axis runs over, the one named last changes fastest.
Arguments:
- courant_sq: float32 [128, 128, 128], P(('groups', 'dom')), parts along dimension 0, may hold values from 0.05 to 0.19
- adjoint_init: float32 [8, 2, 64, 128, 128], P(('groups', 'shot'), None, 'dom'), parts along dimension 0, may hold values from -6 to 6
- forward_saved: bfloat16 [8, 6, 64, 128, 128], P(('groups', 'shot'), None, 'dom'), parts along dimension 0, may hold values from -4 to 4
- residual_traces: float32 [8, 4, 1024], P(('groups', 'shot')), parts along dimension 0, may hold values from -6 to 6
- receivers: int32 [8, 1024, 3], P(('groups', 'shot')), parts along dimension 0, may hold values from 0 to 127, as said below
- sources: int32 [8, 3], P(('groups', 'shot')), parts along dimension 0, may hold values from 0 to 127, as said below
Outputs:
- gradient: float32 [128, 128, 128], P(('groups', 'dom'), 'shot'), parts along dimension 0
- adjoint_final: float32 [8, 2, 64, 128, 128], P(('groups', 'shot'), None, 'dom'), parts along dimension 0
There are 2 independent parts, one for each index of `groups`. A program takes and returns all parts, laid end to end along the dimension named above; each array names one. Nothing has to cross between parts.
Inputs may be any that keep to these rules, and one draw needn't show every extreme that they name: Each row holds the depth index (below 64), the first horizontal index (below 128) and the second (below 128) of a cell; receivers may share cells. `sources`: each row holds the depth index (below 64), the first horizontal index (below 128) and the second (below 128) of a cell.
All inputs are finite; a program needn't handle non-finite values.
Results may differ from a plain program's by a relative error of at most 0.0003.
Values sent between devices are 32-bit elements; how exact they have to be, the bound alone decides.
A program may use at most 64 MiB of HBM per device.

v0:
```python
import functools

import jax
import jax.numpy as jnp
from jax import lax
from jax.experimental import pallas as pl
from jax.experimental.pallas import tpu as pltpu
from jax.sharding import PartitionSpec as P

ITERS = 4
RADIUS = 6
HALO = 4
PAD = 8

STENCIL_WEIGHTS = (-205.0 / 72.0, 8.0 / 5.0, -1.0 / 5.0, 8.0 / 315.0, -1.0 / 560.0)


def kernel(
    dom_n,
    shot_n,
    source_ref,
    spot_ref,
    trace_ref,
    courant_hbm,
    init_hbm,
    fwd_hbm,
    grad_ref,
    final_ref,
    lev,
    courant,
    fwd,
    image,
    hot,
    src,
    band,
    parts,
    in_sem,
    send_sem,
    recv_sem,
    part_send,
    part_recv,
):
    slab, size_x, size_y = courant.shape
    rows = size_x // shot_n
    me = lax.axis_index("dom")
    shot = lax.axis_index("shot")
    has_up = me > 0
    has_down = me < dom_n - 1

    loads = [
        pltpu.make_async_copy(
            init_hbm.at[1], lev.at[1, pl.ds(HALO, slab), pl.ds(PAD, size_x), :], in_sem.at[0]
        ),
        pltpu.make_async_copy(
            init_hbm.at[0], lev.at[0, pl.ds(HALO, slab), pl.ds(PAD, size_x), :], in_sem.at[1]
        ),
        pltpu.make_async_copy(courant_hbm, courant, in_sem.at[2]),
        pltpu.make_async_copy(fwd_hbm, fwd, in_sem.at[3]),
    ]
    for load in loads:
        load.start()

    @pl.when(jnp.logical_not(has_up))
    def _():
        for level in range(1, ITERS + 1):
            lev[level, 0:HALO] = jnp.zeros((HALO, size_x + 2 * PAD, size_y), jnp.float32)

    @pl.when(jnp.logical_not(has_down))
    def _():
        for level in range(1, ITERS + 1):
            lev[level, HALO + slab :] = jnp.zeros((HALO, size_x + 2 * PAD, size_y), jnp.float32)

    barrier = pltpu.get_barrier_semaphore()

    @pl.when(has_up)
    def _():
        pl.semaphore_signal(barrier, inc=1, device_id={"dom": me - 1})

    @pl.when(has_down)
    def _():
        pl.semaphore_signal(barrier, inc=1, device_id={"dom": me + 1})

    for d in range(1, shot_n):
        pl.semaphore_signal(barrier, inc=1, device_id={"shot": lax.rem(shot + d, shot_n)})
    pl.semaphore_wait(
        barrier, has_up.astype(jnp.int32) + has_down.astype(jnp.int32) + (shot_n - 1)
    )

    def owner(i):
        i = i + 1
        if shot_n % 2:
            return lax.rem(shot + i, shot_n)
        pair = lax.rem(lax.div(shot, 2) + (i // 2 + i % 2) % (shot_n // 2), shot_n // 2)
        return pair * 2 + lax.rem(shot + i, 2)

    def halo_copies(step, strip):
        level = step + 1
        begin = pl.multiple_of(owner(strip) * rows, 8)
        cut = pl.ds(pl.multiple_of(PAD + begin, 8), rows)
        if step == 0:
            plain = pl.ds(begin, rows)
            low = init_hbm.at[1, pl.ds(0, HALO), plain, :]
            high = init_hbm.at[1, pl.ds(slab - HALO, HALO), plain, :]
        else:
            low = lev.at[level, pl.ds(HALO, HALO), cut, :]
            high = lev.at[level, pl.ds(slab, HALO), cut, :]
        upward = pltpu.make_async_remote_copy(
            src_ref=low,
            dst_ref=lev.at[level, pl.ds(HALO + slab, HALO), cut, :],
            send_sem=send_sem.at[step, 0, strip],
            recv_sem=recv_sem.at[step, 0, strip],
            device_id={"dom": me - 1},
        )
        downward = pltpu.make_async_remote_copy(
            src_ref=high,
            dst_ref=lev.at[level, pl.ds(0, HALO), cut, :],
            send_sem=send_sem.at[step, 1, strip],
            recv_sem=recv_sem.at[step, 1, strip],
            device_id={"dom": me + 1},
        )
        return upward, downward

    def send_halo(step, strip):
        upward, downward = halo_copies(step, strip)

        @pl.when(has_up)
        def _():
            upward.start()

        @pl.when(has_down)
        def _():
            downward.start()

    def wait_halo(step, strip):
        upward, downward = halo_copies(step, strip)

        @pl.when(has_down)
        def _():
            upward.wait_recv()

        @pl.when(has_up)
        def _():
            downward.wait_recv()

    def wait_sent(step, strip):
        upward, downward = halo_copies(step, strip)

        @pl.when(has_up)
        def _():
            upward.wait_send()

        @pl.when(has_down)
        def _():
            downward.wait_send()

    for strip in range(shot_n):
        send_halo(0, strip)

    for level in range(1, ITERS + 1):
        lev[level, HALO : HALO + slab, 0:PAD] = jnp.zeros((slab, PAD, size_y), jnp.float32)
        lev[level, HALO : HALO + slab, PAD + size_x :] = jnp.zeros(
            (slab, PAD, size_y), jnp.float32
        )
    gap = jnp.abs(
        lax.broadcasted_iota(jnp.int32, (size_y, size_y), 0)
        - lax.broadcasted_iota(jnp.int32, (size_y, size_y), 1)
    )
    weights = jnp.where(gap == 0, jnp.float32(3.0 * STENCIL_WEIGHTS[0]), jnp.float32(0.0))
    for offset in range(1, HALO + 1):
        weights = jnp.where(gap == offset, jnp.float32(STENCIL_WEIGHTS[offset]), weights)
    coarse = weights.astype(jnp.bfloat16)
    band[0:size_y, :] = coarse
    band[size_y : 2 * size_y, :] = coarse
    band[2 * size_y :, :] = (weights - coarse.astype(jnp.float32)).astype(jnp.bfloat16)

    n_rec = spot_ref.shape[2]

    @pl.loop(0, slab)
    def _(z):
        row = lax.broadcasted_iota(jnp.int32, (size_x, n_rec), 0) + z * size_x
        same = row == (spot_ref[0] - me * slab) * size_x + spot_ref[1]
        hot[pl.ds(pl.multiple_of(z * size_x, size_x), size_x), :] = jnp.where(
            same, 1.0, 0.0
        ).astype(jnp.bfloat16)

    def place(section):
        amount = trace_ref[section : section + 1, :]
        high = amount.astype(jnp.bfloat16).astype(jnp.float32)
        low = amount - high
        same = lax.broadcasted_iota(jnp.int32, (size_y, n_rec), 0) == spot_ref[2]
        columns = jnp.concatenate(
            [jnp.where(same, high, 0.0), jnp.where(same, low, 0.0)], axis=0
        ).astype(jnp.bfloat16)
        block = 4 * size_x

        @pl.loop(0, slab * size_x // block)
        def _(i):
            cut = pl.ds(pl.multiple_of(i * block, block), block)
            src[cut, :] = lax.dot_general(
                hot[cut, :],
                columns,
                (((1,), (1,)), ((), ())),
                preferred_element_type=jnp.float32,
            )

    def update(step, z, planes, first, count):
        level = step + 1
        section = ITERS - 1 - step
        cut = pl.ds(PAD + first, count)
        plain = pl.ds(first, count)
        here = pl.ds(z, planes)
        now = lev[level, pl.ds(HALO + z, planes), cut, :]
        flat = now.reshape(planes * count, size_y)
        high = flat.astype(jnp.bfloat16)
        low = (flat - high.astype(jnp.float32)).astype(jnp.bfloat16)
        total = lax.dot_general(
            jnp.concatenate([high, low, high], axis=1),
            band[...],
            (((1,), (0,)), ((), ())),
            preferred_element_type=jnp.float32,
        ).reshape(planes, count, size_y)
        for offset in range(1, HALO + 1):
            beside = (
                lev[level, pl.ds(HALO + z + offset, planes), cut, :]
                + lev[level, pl.ds(HALO + z - offset, planes), cut, :]
                + lev[level, pl.ds(HALO + z, planes), pl.ds(PAD + first + offset, count), :]
                + lev[level, pl.ds(HALO + z, planes), pl.ds(PAD + first - offset, count), :]
            )
            total = total + STENCIL_WEIGHTS[offset] * beside
        added = []
        for p in range(planes):
            at = pl.ds(pl.multiple_of((z + p) * size_x + first, 8), count)
            added.append(src[at, 0:size_y] + src[at, size_y : 2 * size_y])
        added = added[0][None] if planes == 1 else jnp.stack(added)
        later = lev[level - 1, pl.ds(HALO + z, planes), cut, :]
        new = 2.0 * now - later + courant[here, plain, :] * total + added
        if step < ITERS - 1:
            lev[level + 1, pl.ds(HALO + z, planes), cut, :] = new
        if step >= ITERS - 2:
            final_ref[step - (ITERS - 2), here, plain, :] = new
        accel = (
            fwd[section + 2, here, plain, :].astype(jnp.float32)
            - 2.0 * fwd[section + 1, here, plain, :].astype(jnp.float32)
            + fwd[section, here, plain, :].astype(jnp.float32)
        )
        value = new * accel
        if step > 0:
            value = value + image[here, plain, :]
        if step == ITERS - 1:
            shape = (planes, count, size_y)
            dz = lax.broadcasted_iota(jnp.int32, shape, 0) + (me * slab + z - source_ref[0])
            dx = lax.broadcasted_iota(jnp.int32, shape, 1) + (first - source_ref[1])
            dy = lax.broadcasted_iota(jnp.int32, shape, 2) - source_ref[2]
            distance = (dz * dz + dx * dx + dy * dy).astype(jnp.float32)
            value = value * (1.0 - jnp.exp(distance * (-1.0 / float(RADIUS * RADIUS))))
        image[here, plain, :] = value

    paired = shot_n == 4

    def part_copy(i, group):
        first_z, planes = groups[group]
        target = owner(2) if paired and i == 0 else owner(i)
        return pltpu.make_async_remote_copy(
            src_ref=image.at[
                pl.ds(first_z, planes), pl.ds(pl.multiple_of(owner(i) * rows, 8), rows), :
            ],
            dst_ref=parts.at[i, pl.ds(first_z, planes), :, :],
            send_sem=part_send.at[group, i],
            recv_sem=part_recv.at[group, i],
            device_id={"shot": target},
        )

    def part_start(i, group):
        if paired and i == 1:
            first_z, planes = groups[group]
            strip = pl.ds(pl.multiple_of(owner(1) * rows, 8), rows)
            part_copy(0, group).wait_recv()
            here = pl.ds(first_z, planes)
            image[here, strip, :] = image[here, strip, :] + parts[0, here]
        part_copy(i, group).start()

    groups = ((HALO, slab - 2 * HALO), (0, HALO), (slab - HALO, HALO))

    for step in range(ITERS):
        last = step == ITERS - 1
        place(ITERS - 1 - step)
        if step == 0:
            for load in loads:
                load.wait()

        @pl.loop(HALO, slab - HALO, step=HALO)
        def _(z):
            for strip in range(shot_n):
                update(step, z, HALO, strip * rows, rows)

        if last:
            for i in (0, 2, 1) if paired else range(shot_n - 1):
                part_start(i, 0)

        for i in range(shot_n):
            first = pl.multiple_of(owner(i) * rows, 8)
            wait_halo(step, i)
            update(step, 0, HALO, first, rows)
            update(step, slab - HALO, HALO, first, rows)
            if not last:
                send_halo(step + 1, i)
            elif i < shot_n - 1:
                part_start(i, 1)
                part_start(i, 2)

    mine = pl.ds(pl.multiple_of(shot * rows, 8), rows)
    for group in range(3):
        first_z, planes = groups[group]
        value = image[first_z : first_z + planes, mine, :]
        for i in (1, 2) if paired else range(shot_n - 1):
            part_copy(i, group).wait_recv()
            value = value + parts[i, first_z : first_z + planes]
        grad_ref[first_z : first_z + planes] = value

    for step in range(ITERS):
        for i in range(shot_n):
            wait_sent(step, i)
    for group in range(3):
        for i in range(shot_n - 1):
            part_copy(i, group).wait_send()


def per_device(
    dom_n, shot_n, courant_sq, adjoint_init, forward_saved, residual_traces, receivers, sources
):
    slab, size_x, size_y = courant_sq.shape
    n_rec = receivers.shape[1]
    spot = jnp.transpose(receivers, (2, 0, 1))
    hbm = pl.BlockSpec(memory_space=pl.ANY)
    vmem = pl.BlockSpec(memory_space=pltpu.VMEM)
    gradient, final = pl.pallas_call(
        functools.partial(kernel, dom_n, shot_n),
        out_shape=(
            pltpu.VMEM((slab, size_x // shot_n, size_y), jnp.float32),
            pltpu.VMEM((2, slab, size_x, size_y), jnp.float32),
        ),
        in_specs=[pl.BlockSpec(memory_space=pltpu.SMEM), vmem, vmem, hbm, hbm, hbm],
        out_specs=(vmem, vmem),
        scratch_shapes=[
            pltpu.VMEM((ITERS + 2, slab + 2 * HALO, size_x + 2 * PAD, size_y), jnp.float32),
            pltpu.VMEM((slab, size_x, size_y), jnp.float32),
            pltpu.VMEM((ITERS + 2, slab, size_x, size_y), jnp.bfloat16),
            pltpu.VMEM((slab, size_x, size_y), jnp.float32),
            pltpu.VMEM((slab * size_x, n_rec), jnp.bfloat16),
            pltpu.VMEM((slab * size_x, 2 * size_y), jnp.float32),
            pltpu.VMEM((3 * size_y, size_y), jnp.bfloat16),
            pltpu.VMEM((shot_n - 1, slab, size_x // shot_n, size_y), jnp.float32),
            pltpu.SemaphoreType.DMA((4,)),
            pltpu.SemaphoreType.DMA((ITERS, 2, shot_n)),
            pltpu.SemaphoreType.DMA((ITERS, 2, shot_n)),
            pltpu.SemaphoreType.DMA((3, shot_n - 1)),
            pltpu.SemaphoreType.DMA((3, shot_n - 1)),
        ],
        compiler_params=pltpu.CompilerParams(
            collective_id=0, has_side_effects=True, vmem_limit_bytes=60 * 1024 * 1024
        ),
    )(
        sources[0],
        spot,
        residual_traces[0],
        courant_sq,
        adjoint_init[0],
        forward_saved[0],
    )
    return gradient, final[None]


def solution(mesh):
    placed = (
        P(("groups", "dom"), None, None),
        P(("groups", "shot"), None, "dom", None, None),
        P(("groups", "shot"), None, "dom", None, None),
        P(("groups", "shot"), None, None),
        P(("groups", "shot"), None, None),
        P(("groups", "shot"), None),
    )
    return jax.shard_map(
        functools.partial(per_device, mesh.shape["dom"], mesh.shape["shot"]),
        mesh=mesh,
        in_specs=placed,
        out_specs=(
            P(("groups", "dom"), "shot", None),
            P(("groups", "shot"), None, "dom", None, None),
        ),
        check_vma=False,
    )
```

profile of v0, /device:TPU:0, one launch (start us, length us, event | category | flops | bytes accessed | tf_op | source)
XLA Modules:
  0.0 38.6 jit_solution(14481337686025030790)
XLA Ops:
  0.6 35.9 %shard_map.77 = (f32[16,32,128]{2,1,0:T(8,128)S(1)}, f32[2,16,128,128]{3,2,1,0:T(8,128)S(1)}) custom-call(s32[3]{0:T(128)} %bitcast.11, s32[3,1,1024]{2,1,0:T(1,128)} %bitcast.10, f32[4,1024]{1,0:T(4,128)} %bitcast.9, f32[16,128,128]{2,1,0:T(8,128)} %courant_hbm.1, f32[2,16,128,128]{3,2,1,0:T(8,128)} %bitcast.8, bf16[6,16,128,128]{3,2,1,0:T(8,128)(2,1)} %bitcast.7), custom_call_target="tpu_custom_call" | custom-call | tf_op jit(solution)/shard_map/pallas_call | solution.py:336
  36.5 0.7 %copy.10 = f32[16,32,128]{2,1,0:T(8,128)} copy(f32[16,32,128]{2,1,0:T(8,128)S(1)} %get-tuple-element.6) | data formatting | bytes 524288
  37.3 1.3 %copy.11 = f32[1,2,16,128,128]{4,3,2,1,0:T(8,128)} copy(f32[1,2,16,128,128]{4,3,2,1,0:T(8,128)S(1)} %bitcast.6) | data formatting | bytes 4194304
where the time goes:
time: 38.8 us; the launch traced here: 38.6 us
  Pallas kernels  35.9 us (93%)
  local copies, waits for them, and re-layouts  2.02 us (5%)
  between operations  0.64 us (2%)
    pallas_call x1, Pallas kernels, per_device(): pl.pallas_call(functools.partial(kernel, dom_n, shot_n), out_shape=(pltpu...  35.9 us
    unnamed x2, local copies, waits for them, and re-layouts  2.02 us

commit v1 on v0

v1 whole, which is shorter than its diff:
```python
import functools

import jax
import jax.numpy as jnp
from jax import lax
from jax.experimental import pallas as pl
from jax.experimental.pallas import tpu as pltpu
from jax.sharding import PartitionSpec as P

ITERS = 4
RADIUS = 6
HALO = 4
PAD = 8

STENCIL_WEIGHTS = (-205.0 / 72.0, 8.0 / 5.0, -1.0 / 5.0, 8.0 / 315.0, -1.0 / 560.0)


def pieces_of(shot_n, rows):
    if shot_n == 4 and rows % 16 == 0:
        half = rows // 2
        return [(0, 0, half), (1, 0, half), (0, half, half), (1, half, half), (2, 0, rows), (3, 0, rows)]
    return [(i, 0, rows) for i in range(shot_n)]


def kernel(
    dom_n,
    shot_n,
    source_hbm,
    spot_hbm,
    trace_hbm,
    courant_hbm,
    init_hbm,
    fwd_hbm,
    grad_ref,
    final_ref,
    lev,
    courant,
    fwd,
    image,
    hot,
    columns,
    src,
    band,
    parts,
    source,
    spot,
    trace,
    in_sem,
    send_sem,
    recv_sem,
    part_recv,
):
    slab, size_x, size_y = courant.shape
    rows = size_x // shot_n
    n_rec = spot.shape[2]
    inner = slab - 2 * HALO
    pieces = pieces_of(shot_n, rows)
    me = lax.axis_index("dom")
    shot = lax.axis_index("shot")
    has_up = me > 0
    has_down = me < dom_n - 1
    paired = shot_n == 4

    def owner(i):
        i = i + 1
        if shot_n % 2:
            return lax.rem(shot + i, shot_n)
        pair = lax.rem(lax.div(shot, 2) + (i // 2 + i % 2) % (shot_n // 2), shot_n // 2)
        return pair * 2 + lax.rem(shot + i, 2)

    def target(i):
        return owner(2) if paired and i == 0 else owner(i)

    peers = (1, 2) if paired else range(shot_n - 1)
    barrier = pltpu.get_barrier_semaphore()

    @pl.when(has_up)
    def _():
        pl.semaphore_signal(barrier, inc=1, device_id={"dom": me - 1})

    @pl.when(has_down)
    def _():
        pl.semaphore_signal(barrier, inc=1, device_id={"dom": me + 1})

    for i in peers:
        pl.semaphore_signal(barrier, inc=1, device_id={"shot": owner(i)})

    across = pl.ds(PAD, size_x)

    def load_planes(first, count, sem):
        return pltpu.make_async_copy(
            init_hbm.at[1, pl.ds(first, count)],
            lev.at[1, pl.ds(HALO + first, count), across, :],
            in_sem.at[sem],
        )

    edge_loads = [load_planes(0, HALO, 0), load_planes(slab - HALO, HALO, 1)]
    spot_loads = [
        pltpu.make_async_copy(spot_hbm, spot, in_sem.at[2]),
        pltpu.make_async_copy(trace_hbm, trace, in_sem.at[3]),
    ]
    loads = [
        load_planes(HALO, inner, 4),
        pltpu.make_async_copy(init_hbm.at[0], lev.at[0, pl.ds(HALO, slab), across, :], in_sem.at[5]),
        pltpu.make_async_copy(courant_hbm, courant, in_sem.at[6]),
        pltpu.make_async_copy(fwd_hbm, fwd, in_sem.at[7]),
        pltpu.make_async_copy(source_hbm, source, in_sem.at[8]),
    ]
    for load in edge_loads + spot_loads + loads:
        load.start()

    gap = jnp.abs(
        lax.broadcasted_iota(jnp.int32, (size_y, size_y), 0)
        - lax.broadcasted_iota(jnp.int32, (size_y, size_y), 1)
    )
    weights = jnp.where(gap == 0, jnp.float32(3.0 * STENCIL_WEIGHTS[0]), jnp.float32(0.0))
    for offset in range(1, HALO + 1):
        weights = jnp.where(gap == offset, jnp.float32(STENCIL_WEIGHTS[offset]), weights)
    coarse = weights.astype(jnp.bfloat16)
    band[0:size_y, :] = coarse
    band[size_y : 2 * size_y, :] = coarse
    band[2 * size_y :, :] = (weights - coarse.astype(jnp.float32)).astype(jnp.bfloat16)

    for level in range(1, ITERS + 1):
        lev[level, HALO : HALO + slab, 0:PAD] = jnp.zeros((slab, PAD, size_y), jnp.float32)
        lev[level, HALO : HALO + slab, PAD + size_x :] = jnp.zeros(
            (slab, PAD, size_y), jnp.float32
        )

    def span(piece):
        strip, offset, count = pieces[piece]
        return pl.multiple_of(owner(strip) * rows + offset, 8), count

    def halo_copies(step, piece):
        level = step + 1
        first, count = span(piece)
        cut = pl.ds(pl.multiple_of(PAD + first, 8), count)
        upward = pltpu.make_async_remote_copy(
            src_ref=lev.at[level, pl.ds(HALO, HALO), cut, :],
            dst_ref=lev.at[level, pl.ds(HALO + slab, HALO), cut, :],
            send_sem=send_sem.at[0],
            recv_sem=recv_sem.at[step % 2, 0, piece],
            device_id={"dom": me - 1},
        )
        downward = pltpu.make_async_remote_copy(
            src_ref=lev.at[level, pl.ds(slab, HALO), cut, :],
            dst_ref=lev.at[level, pl.ds(0, HALO), cut, :],
            send_sem=send_sem.at[1],
            recv_sem=recv_sem.at[step % 2, 1, piece],
            device_id={"dom": me + 1},
        )
        return upward, downward

    def send_halo(step, piece):
        upward, downward = halo_copies(step, piece)

        @pl.when(has_up)
        def _():
            upward.start()

        @pl.when(has_down)
        def _():
            downward.start()

    def wait_halo(step, piece):
        upward, downward = halo_copies(step, piece)

        @pl.when(has_down)
        def _():
            upward.wait_recv()

        @pl.when(has_up)
        def _():
            downward.wait_recv()

    with jax.named_scope("edge_loads"):
        for load in edge_loads:
            load.wait()
    with jax.named_scope("barrier_wait"):
        pl.semaphore_wait(barrier, has_up.astype(jnp.int32) + has_down.astype(jnp.int32) + len(peers))
    for piece in range(len(pieces)):
        send_halo(0, piece)

    @pl.when(jnp.logical_not(has_up))
    def _():
        for level in range(1, ITERS + 1):
            lev[level, 0:HALO] = jnp.zeros((HALO, size_x + 2 * PAD, size_y), jnp.float32)

    @pl.when(jnp.logical_not(has_down))
    def _():
        for level in range(1, ITERS + 1):
            lev[level, HALO + slab :] = jnp.zeros((HALO, size_x + 2 * PAD, size_y), jnp.float32)

    for load in spot_loads:
        load.wait()

    with jax.named_scope("hot"):

        @pl.loop(0, slab)
        def _(z):
            row = lax.broadcasted_iota(jnp.int32, (size_x, n_rec), 0) + z * size_x
            same = row == (spot[0] - me * slab) * size_x + spot[1]
            hot[pl.ds(pl.multiple_of(z * size_x, size_x), size_x), :] = jnp.where(
                same, 1.0, 0.0
            ).astype(jnp.bfloat16)

        same = lax.broadcasted_iota(jnp.int32, (size_y, n_rec), 0) == spot[2]
        for section in range(ITERS):
            amount = trace[section : section + 1, :]
            high = amount.astype(jnp.bfloat16).astype(jnp.float32)
            columns[section, 0:size_y] = jnp.where(same, high, 0.0).astype(jnp.bfloat16)
            columns[section, size_y:] = jnp.where(same, amount - high, 0.0).astype(jnp.bfloat16)

    block = HALO * size_x
    blocks = slab // HALO

    def place(step, i):
        cut = pl.ds(pl.multiple_of(i * block, block), block)
        both = lax.dot_general(
            hot[cut, :],
            columns[ITERS - 1 - step],
            (((1,), (1,)), ((), ())),
            preferred_element_type=jnp.float32,
        )
        src[step, cut, :] = both[:, 0:size_y] + both[:, size_y:]

    def update(step, z, first, count, at):
        level = step + 1
        section = ITERS - 1 - step
        planes = HALO
        cut = pl.ds(pl.multiple_of(PAD + first, 8), count)
        plain = pl.ds(first, count)
        here = pl.ds(z, planes)
        store = pl.ds(at, planes)
        now = lev[level, pl.ds(HALO + z, planes), cut, :]
        flat = now.reshape(planes * count, size_y)
        high = flat.astype(jnp.bfloat16)
        low = (flat - high.astype(jnp.float32)).astype(jnp.bfloat16)
        total = lax.dot_general(
            jnp.concatenate([high, low, high], axis=1),
            band[...],
            (((1,), (0,)), ((), ())),
            preferred_element_type=jnp.float32,
        ).reshape(planes, count, size_y)
        for offset in range(1, HALO + 1):
            beside = (
                lev[level, pl.ds(HALO + z + offset, planes), cut, :]
                + lev[level, pl.ds(HALO + z - offset, planes), cut, :]
                + lev[level, pl.ds(HALO + z, planes), pl.ds(PAD + first + offset, count), :]
                + lev[level, pl.ds(HALO + z, planes), pl.ds(PAD + first - offset, count), :]
            )
            total = total + STENCIL_WEIGHTS[offset] * beside
        added = [
            src[step, pl.ds(pl.multiple_of((z + p) * size_x + first, 8), count), :]
            for p in range(planes)
        ]
        later = lev[level - 1, pl.ds(HALO + z, planes), cut, :]
        new = 2.0 * now - later + courant[here, plain, :] * total + jnp.stack(added)
        if step < ITERS - 1:
            lev[level + 1, pl.ds(HALO + z, planes), cut, :] = new
        if step >= ITERS - 2:
            final_ref[step - (ITERS - 2), here, plain, :] = new
        accel = (
            fwd[section + 2, here, plain, :].astype(jnp.float32)
            - 2.0 * fwd[section + 1, here, plain, :].astype(jnp.float32)
            + fwd[section, here, plain, :].astype(jnp.float32)
        )
        value = new * accel
        if step > 0:
            value = value + image[store, plain, :]
        if step == ITERS - 1:
            shape = (planes, count, size_y)
            dz = lax.broadcasted_iota(jnp.int32, shape, 0) + (me * slab + z - source[0])
            dx = lax.broadcasted_iota(jnp.int32, shape, 1) + (first - source[1])
            dy = lax.broadcasted_iota(jnp.int32, shape, 2) - source[2]
            distance = (dz * dz + dx * dx + dy * dy).astype(jnp.float32)
            value = value * (1.0 - jnp.exp(distance * (-1.0 / float(RADIUS * RADIUS))))
        image[store, plain, :] = value

    def interior(step, strips):
        @pl.loop(HALO, slab - HALO, step=HALO)
        def _(z):
            for strip in strips:
                first = pl.multiple_of(owner(strip) * rows, 8)
                update(step, z, first, rows, z + HALO)

    def edges(step, piece):
        first, count = span(piece)
        update(step, 0, first, count, 0)
        update(step, slab - HALO, first, count, HALO)

    def part_copy(slot, strip, at, planes, offset, count):
        return pltpu.make_async_remote_copy(
            src_ref=image.at[
                pl.ds(at, planes), pl.ds(pl.multiple_of(owner(strip) * rows + offset, 8), count), :
            ],
            dst_ref=parts.at[strip, pl.ds(at, planes), pl.ds(offset, count), :],
            send_sem=send_sem.at[2],
            recv_sem=part_recv.at[slot],
            device_id={"shot": target(strip)},
        )

    inner_parts = [part_copy(i, i, 2 * HALO, inner, 0, rows) for i in range(shot_n - 1)]
    edge_parts = {
        piece: part_copy(shot_n - 1 + piece, strip, 0, 2 * HALO, offset, count)
        for piece, (strip, offset, count) in enumerate(pieces)
        if strip < shot_n - 1
    }

    def relay(at, planes, offset, count, arrived, onward):
        arrived.wait_recv()
        here = pl.ds(at, planes)
        cut = pl.ds(pl.multiple_of(owner(1) * rows + offset, 8), count)
        image[here, cut, :] = image[here, cut, :] + parts[0, here, pl.ds(offset, count), :]
        onward.start()

    for i in range(blocks):
        with jax.named_scope("place0"):
            place(0, i)
    for load in loads:
        load.wait()

    half = shot_n // 2
    strips = list(range(shot_n))
    for step in range(ITERS - 1):
        jobs = [[] for _ in pieces]
        jobs[0].append(functools.partial(interior, step, strips[:half]))
        jobs[1 % len(pieces)].append(functools.partial(interior, step, strips[half:]))
        for i in range(blocks):
            jobs[min(2 + i, max(len(pieces) - 2, 0))].append(functools.partial(place, step + 1, i))
        for piece in range(len(pieces)):
            with jax.named_scope(f"wait{step}_{piece}"):
                wait_halo(step, piece)
            edges(step, piece)
            send_halo(step + 1, piece)
            with jax.named_scope(f"jobs{step}_{piece}"):
                for job in jobs[piece]:
                    job()

    step = ITERS - 1
    with jax.named_scope("interior3"):
        if paired:
            interior(step, [0])
            inner_parts[0].start()
            interior(step, [1, 2])
            inner_parts[2].start()
            interior(step, [3])
            relay(2 * HALO, inner, 0, rows, inner_parts[0], inner_parts[1])
        else:
            for i in range(shot_n):
                interior(step, [i])
                if i < shot_n - 1:
                    inner_parts[i].start()

    pending = []
    for piece, (strip, offset, count) in enumerate(pieces):
        with jax.named_scope(f"wait{step}_{piece}"):
            wait_halo(step, piece)
        edges(step, piece)
        if strip < shot_n - 1 and not (paired and strip == 1):
            edge_parts[piece].start()
        if paired and strip == 1:
            pending.append(piece)
        if paired and (strip == 0 or piece == max(p for p in edge_parts if pieces[p][0] == 1)):
            while pending:
                onward = pending.pop(0)
                _, offset, count = pieces[onward]
                with jax.named_scope(f"relay{onward}"):
                    relay(0, 2 * HALO, offset, count, edge_parts[pieces.index((0, offset, count))], edge_parts[onward])

    mine = pl.multiple_of(shot * rows, 8)
    adding = (2, 1) if paired else range(shot_n - 1)

    def finish(at, planes, z, offset, count):
        value = image[pl.ds(at, planes), pl.ds(pl.multiple_of(mine + offset, 8), count), :]
        for i in adding:
            value = value + parts[i, pl.ds(at, planes), pl.ds(offset, count), :]
        grad_ref[pl.ds(z, planes), pl.ds(offset, count), :] = value

    with jax.named_scope("final_inner"):
        for i in adding:
            inner_parts[i].wait_recv()
        finish(2 * HALO, inner, HALO, 0, rows)
    with jax.named_scope("final_edge"):
        for i in adding:
            for piece in edge_parts:
                if pieces[piece][0] == i:
                    edge_parts[piece].wait_recv()
        finish(0, HALO, 0, 0, rows)
        finish(HALO, HALO, slab - HALO, 0, rows)

    whole = lev.at[0, pl.ds(0, ITERS * HALO), across, :]
    sent = [
        pltpu.make_async_remote_copy(
            src_ref=whole,
            dst_ref=whole,
            send_sem=send_sem.at[i],
            recv_sem=recv_sem.at[0, i, 0],
            device_id={"dom": me + 2 * i - 1},
        )
        for i in range(2)
    ]

    @pl.when(has_up)
    def _():
        sent[0].wait_send()

    @pl.when(has_down)
    def _():
        sent[1].wait_send()

    pltpu.make_async_remote_copy(
        src_ref=parts,
        dst_ref=parts,
        send_sem=send_sem.at[2],
        recv_sem=part_recv.at[0],
        device_id={"shot": owner(0)},
    ).wait_send()


def flush(grad_ref, final_ref, grad_out, final_out, sem):
    copies = [pltpu.make_async_copy(grad_ref, grad_out, sem.at[0])]
    for i in range(final_ref.shape[0]):
        copies.append(pltpu.make_async_copy(final_ref.at[i], final_out.at[i], sem.at[1 + i]))
    for copy in copies:
        copy.start()
    for copy in copies:
        copy.wait()


def per_device(
    dom_n, shot_n, courant_sq, adjoint_init, forward_saved, residual_traces, receivers, sources
):
    slab, size_x, size_y = courant_sq.shape
    n_rec = receivers.shape[1]
    rows = size_x // shot_n
    pieces = pieces_of(shot_n, rows)
    spot = jnp.transpose(receivers, (2, 0, 1))
    hbm = pl.BlockSpec(memory_space=pl.ANY)
    vmem = pl.BlockSpec(memory_space=pltpu.VMEM)
    gradient, final = pl.pallas_call(
        functools.partial(kernel, dom_n, shot_n),
        out_shape=(
            pltpu.VMEM((slab, rows, size_y), jnp.float32),
            pltpu.VMEM((2, slab, size_x, size_y), jnp.float32),
        ),
        in_specs=[hbm] * 6,
        out_specs=(vmem, vmem),
        scratch_shapes=[
            pltpu.VMEM((ITERS + 1, slab + 2 * HALO, size_x + 2 * PAD, size_y), jnp.float32),
            pltpu.VMEM((slab, size_x, size_y), jnp.float32),
            pltpu.VMEM((ITERS + 2, slab, size_x, size_y), jnp.bfloat16),
            pltpu.VMEM((slab, size_x, size_y), jnp.float32),
            pltpu.VMEM((slab * size_x, n_rec), jnp.bfloat16),
            pltpu.VMEM((ITERS, 2 * size_y, n_rec), jnp.bfloat16),
            pltpu.VMEM((ITERS, slab * size_x, size_y), jnp.float32),
            pltpu.VMEM((3 * size_y, size_y), jnp.bfloat16),
            pltpu.VMEM((shot_n - 1, slab, rows, size_y), jnp.float32),
            pltpu.SMEM(sources.shape[1:], jnp.int32),
            pltpu.VMEM(spot.shape, jnp.int32),
            pltpu.VMEM(residual_traces.shape[1:], jnp.float32),
            pltpu.SemaphoreType.DMA((9,)),
            pltpu.SemaphoreType.DMA((3,)),
            pltpu.SemaphoreType.DMA((2, 2, len(pieces))),
            pltpu.SemaphoreType.DMA((shot_n - 1 + len(pieces),)),
        ],
        compiler_params=pltpu.CompilerParams(
            collective_id=0, has_side_effects=True, vmem_limit_bytes=56 * 1024 * 1024
        ),
    )(
        sources[0],
        spot,
        residual_traces[0],
        courant_sq,
        adjoint_init[0],
        forward_saved[0],
    )
    gradient, final = pl.pallas_call(
        flush,
        out_shape=(
            jax.ShapeDtypeStruct(gradient.shape, jnp.float32),
            jax.ShapeDtypeStruct(final.shape, jnp.float32),
        ),
        in_specs=[vmem, vmem],
        out_specs=(hbm, hbm),
        scratch_shapes=[pltpu.SemaphoreType.DMA((3,))],
        compiler_params=pltpu.CompilerParams(vmem_limit_bytes=1024 * 1024),
    )(gradient, final)
    return gradient, final[None]


def solution(mesh):
    placed = (
        P(("groups", "dom"), None, None),
        P(("groups", "shot"), None, "dom", None, None),
        P(("groups", "shot"), None, "dom", None, None),
        P(("groups", "shot"), None, None),
        P(("groups", "shot"), None, None),
        P(("groups", "shot"), None),
    )
    return jax.shard_map(
        functools.partial(per_device, mesh.shape["dom"], mesh.shape["shot"]),
        mesh=mesh,
        in_specs=placed,
        out_specs=(
            P(("groups", "dom"), "shot", None),
            P(("groups", "shot"), None, "dom", None, None),
        ),
        check_vma=False,
    )
```

time: 38.8 us -> 35.7 us (0.920)
  local copies, waits for them, and re-layouts: 2.02 us -> 0 us
  Pallas kernels: 35.9 us -> 34.9 us
    pallas_call x1, Pallas kernels: 35.9 us -> 33.5 us  [per_device(): pl.pallas_call(functools.partial(kernel, dom_n, shot_n), out_shape=(pltpu...]
    unnamed x2 -> x0, local copies, waits for them, and re-layouts: 2.02 us -> none
    pallas_call x0 -> x1, Pallas kernels: none -> 1.43 us  [per_device(): pl.pallas_call(flush, out_shape=(jax.ShapeDtypeStruct(gradient.shape, jnp...]
where the time goes in v1:
time: 35.7 us; the launch traced here: 35.5 us
  Pallas kernels  34.9 us (98%)
  between operations  0.64 us (2%)
    pallas_call x1, Pallas kernels, per_device(): pl.pallas_call(functools.partial(kernel, dom_n, shot_n), out_shape=(pltpu...  33.5 us
    pallas_call x1, Pallas kernels, per_device(): pl.pallas_call(flush, out_shape=(jax.ShapeDtypeStruct(gradient.shape, jnp...  1.43 us

profile of v1, /device:TPU:0, one launch (start us, length us, event | category | flops | bytes accessed | tf_op | source)
XLA Modules:
  0.0 35.5 jit_solution(7232998781807834441)
XLA Ops:
  0.6 33.5 %shard_map.77 = (f32[16,32,128]{2,1,0:T(8,128)S(1)}, f32[2,16,128,128]{3,2,1,0:T(8,128)S(1)}) custom-call(s32[3]{0:T(128)} %bitcast.10, s32[3,1,1024]{2,1,0:T(1,128)} %bitcast.9, f32[4,1024]{1,0:T(4,128)} %bitcast.8, f32[16,128,128]{2,1,0:T(8,128)} %courant_hbm.1, f32[2,16,128,128]{3,2,1,0:T(8,128)} %bitcast.7, bf16[6,16,128,128]{3,2,1,0:T(8,128)(2,1)} %bitcast.6), custom_call_target="tpu_custom_call" | custom-call | tf_op jit(solution)/shard_map/pallas_call | solution.py:441
  34.1 1.4 %shard_map.78 = (f32[16,32,128]{2,1,0:T(8,128)}, f32[2,16,128,128]{3,2,1,0:T(8,128)}) custom-call(f32[16,32,128]{2,1,0:T(8,128)S(1)} %get-tuple-element.6.grad_ref, f32[2,16,128,128]{3,2,1,0:T(8,128)S(1)} %get-tuple-element.7.final_ref), custom_call_target="tpu_custom_call" | custom-call | tf_op jit(solution)/shard_map/pallas_call | solution.py:478
